TPU v7x, 32 devices: a whole 2x2x4 slice. The times are simulated.
32 devices in a mesh: groups: 2 (over x), tp: 8 (over z, y), role: 2 (over core).
Axes of the slice: x: 2, y: 2, z: 4, core: 2. Of those that a mesh axis runs over, the one named last changes fastest.
Arguments:
- rows_in: bfloat16 [2, 1024, 8192], P('role', 'groups', 'tp'), parts along dimension 1, may hold values from -6 to 6
- norm_gain: bfloat16 [8192], replicated, may hold values from 0.5 to 4
- q_words: int32 [1024, 8192], P(None, 'tp'), may hold values from -2147483648 to 2147483646
- q_scales: bfloat16 [64, 8192], P(None, 'tp'), may hold values from 0.0011978149 to 0.0047912598
- kv_words: int32 [8, 1024, 256], P('tp'), may hold values from -2147483648 to 2147483646, as said below
- kv_scales: bfloat16 [8, 64, 256], P('tp'), may hold values from 0.0012 to 0.0048, as said below
- o_words: int32 [1024, 8192], P('tp'), may hold values from -2147483648 to 2147483646
- o_scales: bfloat16 [64, 8192], P('tp'), may hold values from 0.0011978149 to 0.0047912598
- kv_pool: bfloat16 [8, 2048, 16, 256], P('tp', 'groups'), parts along dimension 1, may hold values from -120 to 120, as said below
- prompt_pages: int32 [32], P('groups'), parts along dimension 0, may hold values from 1 to 8, 32 in all
- page_slots: int32 [64], P('groups'), parts along dimension 0, may hold values from 0 to 1023, as said below
- block_tables: int32 [992, 16], P('groups'), parts along dimension 0, may hold values from 0 to 1023, as said below
- cache_lens: int32 [992], P('groups'), parts along dimension 0, may hold values from 1 to 256
Outputs:
- layer_out: bfloat16 [2, 1024, 8192], P('role', 'groups', 'tp'), parts along dimension 1
There are 2 independent parts, one for each index of `groups`. A program takes and returns all parts, laid end to end along the dimension named above; an argument that names none is the same for every part. Nothing has to cross between parts.
Inputs may be any that keep to these rules, and one draw needn't show every extreme that they name: `kv_words`: entries t and u are equal whenever t * 8 // 8 equals u * 8 // 8. `kv_scales`: entries t and u are equal whenever t * 8 // 8 equals u * 8 // 8. `kv_pool`: entries t and u are equal whenever t * 8 // 8 equals u * 8 // 8. `page_slots`: distinct pages; entry j receives the j-th page of the prompts taken in order. `block_tables`: no entry is one of page_slots; sequences may share pages.
All inputs are finite; a program needn't handle non-finite values.
Results may differ from a plain program's by a relative error of at most 0.015.
The roundings to bfloat16 on the way count: a program that leaves them out, or rounds other values in their place, can miss the bound.
Values may be sent and summed in bfloat16 or wider, within the bound.
A program may use at most 192 MiB of HBM per device.

v0:
```python
import jax
import jax.numpy as jnp
from jax import lax
from jax.sharding import PartitionSpec as P

HD = 128


def passed_along(block, axis, distance):
    devices = range(lax.axis_size(axis))
    route = [(i - distance, i) for i in devices if i - distance in devices]
    return lax.ppermute(block, axis, route)


def unpack_words(words, scales):
    shifts = jnp.arange(8, dtype=jnp.int32) * 4
    nibbles = jnp.bitwise_and(jnp.right_shift(words[:, None, :], shifts[None, :, None]), 15) - 8
    values = nibbles.reshape(words.shape[0] * 8, words.shape[1]).astype(jnp.float32)
    group = values.shape[0] // scales.shape[0]
    spread = jnp.repeat(scales.astype(jnp.float32), group, axis=0)
    return (values * spread).astype(jnp.bfloat16)


def rms_normed(rows, gain):
    wide = rows.astype(jnp.float32)
    inverse = lax.rsqrt(jnp.mean(wide * wide, axis=-1, keepdims=True) + 1e-05)
    return (wide * inverse * gain.astype(jnp.float32)).astype(jnp.bfloat16)


def rotate(heads, positions):
    half = heads.shape[-1] // 2
    freq = 500000.0 ** (-jnp.arange(half, dtype=jnp.float32) * 2.0 / heads.shape[-1])
    angle = positions.astype(jnp.float32)[:, None, None] * freq[None, None, :]
    cosine = jnp.cos(angle)
    sine = jnp.sin(angle)
    first = heads[..., :half]
    second = heads[..., half:]
    return jnp.concatenate(
        [first * cosine - second * sine, second * cosine + first * sine], axis=-1
    )


def layout(prompt_pages, page_slots, block_tables, cache_lens, rows):
    page = rows // page_slots.shape[0]
    count = prompt_pages.shape[0]
    ends = jnp.cumsum(prompt_pages) * page
    starts = ends - prompt_pages * page
    index = jnp.arange(rows, dtype=jnp.int32)
    member = (index[:, None] >= starts[None, :]) & (index[:, None] < ends[None, :])
    doc = jnp.sum(jnp.where(member, jnp.arange(count, dtype=jnp.int32)[None, :], 0), axis=1)
    prefill_pos = index - jnp.sum(jnp.where(member, starts[None, :], 0), axis=1)
    span = block_tables.shape[1]
    picks = jnp.minimum(
        starts[:, None] // page + jnp.arange(span, dtype=jnp.int32)[None, :],
        page_slots.shape[0] - 1,
    )
    prompt_table = page_slots[picks]
    table = jnp.concatenate([prompt_table, block_tables], axis=0)
    lengths = jnp.concatenate([prompt_pages * page, cache_lens])
    return (doc, prefill_pos, table, lengths)


def prefill_attend(query, keys, values, doc):
    rows = query.shape[0]
    block = min(512, rows)
    score_scale = query.shape[-1] ** (-0.5)
    index = jnp.arange(rows, dtype=jnp.int32)

    def prefill_one_block(start):
        logit_scores = (
            jnp.einsum("qhd,kd->hqk", query, keys, preferred_element_type=jnp.float32) * score_scale
        )
        own = start + jnp.arange(block, dtype=jnp.int32)
        allowed = (doc[:, None] == doc[None, :]) & (index[None, :] <= own[:, None])
        logit_scores = jnp.where(allowed[None], logit_scores, -1e30)
        attention_probs = jax.nn.softmax(logit_scores, axis=-1).astype(jnp.bfloat16)
        return jnp.einsum(
            "hqk,kd->qhd", attention_probs, values, preferred_element_type=jnp.float32
        ).astype(jnp.bfloat16)

    starts = jnp.arange(0, rows, block, dtype=jnp.int32)
    done = lax.map(prefill_one_block, starts)
    return done.reshape(rows, query.shape[1], query.shape[2])


def decode_attend(query, key_self, value_self, cache, table, lengths):
    rows = query.shape[0]
    block = min(128, rows)
    score_scale = query.shape[-1] ** (-0.5)
    head_dim = query.shape[-1]

    def decode_one_block(start):
        partial_query = lax.dynamic_slice_in_dim(query, start, block, 0)
        part_table = lax.dynamic_slice_in_dim(table, start, block, 0)
        part_len = lax.dynamic_slice_in_dim(lengths, start, block, 0)
        pages = cache[part_table]
        pages = pages.reshape(block, pages.shape[1] * pages.shape[2], pages.shape[3])
        own_key = lax.dynamic_slice_in_dim(key_self, start, block, 0)
        own_value = lax.dynamic_slice_in_dim(value_self, start, block, 0)
        gathered_keys = jnp.concatenate([pages[..., :head_dim], own_key[:, None, :]], axis=1)
        gathered_values = jnp.concatenate([pages[..., head_dim:], own_value[:, None, :]], axis=1)
        logit_scores = (
            jnp.einsum(
                "jai,jri->jar", partial_query, gathered_keys, preferred_element_type=jnp.float32
            )
            * score_scale
        )
        spots = jnp.arange(pages.shape[1], dtype=jnp.int32)
        valid = jnp.concatenate(
            [spots[None, :] < part_len[:, None], jnp.ones((block, 1), dtype=bool)], axis=1
        )
        logit_scores = jnp.where(valid[:, None, :], logit_scores, -1e30)
        attention_probs = jax.nn.softmax(logit_scores, axis=-1).astype(jnp.bfloat16)
        return jnp.einsum(
            "cwt,ctr->cwr", attention_probs, gathered_values, preferred_element_type=jnp.float32
        ).astype(jnp.bfloat16)

    starts = jnp.arange(0, rows, block, dtype=jnp.int32)
    done = lax.map(decode_one_block, starts)
    return done.reshape(rows, query.shape[1], query.shape[2])


def local(
    rows_in,
    norm_gain,
    q_words,
    q_scales,
    kv_words,
    kv_scales,
    o_words,
    o_scales,
    kv_pool,
    prompt_pages,
    page_slots,
    block_tables,
    cache_lens,
):
    side = lax.axis_index("role")
    whole = lax.all_gather(rows_in[0], "tp", axis=1, tiled=True)
    rows = whole.shape[0]
    normed = rms_normed(whole, norm_gain)
    doc, prefill_pos, table, lengths = layout(
        prompt_pages, page_slots, block_tables, cache_lens, rows
    )
    positions = jnp.where(side == 0, prefill_pos, lengths)
    w_query = unpack_words(q_words, q_scales)
    w_keyval = unpack_words(kv_words[0], kv_scales[0])
    projected = jnp.dot(normed, w_query, preferred_element_type=jnp.float32)
    query = rotate(projected.reshape(rows, -1, HD), positions).astype(jnp.bfloat16)
    keyval = jnp.dot(normed, w_keyval, preferred_element_type=jnp.float32)
    key_new = rotate(keyval[:, None, :HD], positions)[:, 0].astype(jnp.bfloat16)
    value_new = keyval[:, HD:].astype(jnp.bfloat16)
    fresh = jnp.concatenate([key_new, value_new], axis=1)
    arrived = passed_along(fresh, "role", 1)
    pool = kv_pool[0]

    def run_prefill():
        return prefill_attend(query, key_new, value_new, doc)

    def run_decode():
        cache = pool.at[page_slots].set(arrived.reshape(-1, pool.shape[1], pool.shape[2]))
        return decode_attend(query, key_new, value_new, cache, table, lengths)

    attention_output = lax.cond(side == 0, run_prefill, run_decode).reshape(rows, -1)
    column_words, column_scales = (
        lax.all_to_all(o_words, "tp", split_axis=1, concat_axis=0, tiled=True),
        lax.all_to_all(o_scales, "tp", split_axis=1, concat_axis=0, tiled=True),
    )
    w_columns = unpack_words(column_words, column_scales)
    summed = jnp.dot(
        lax.all_gather(attention_output, "tp", axis=1, tiled=True),
        w_columns,
        preferred_element_type=jnp.float32,
    )
    return summed.astype(jnp.bfloat16)[None]


def solution(mesh):
    return jax.shard_map(
        local,
        mesh=mesh,
        in_specs=(
            P("role", "groups", "tp"),
            P(),
            P(None, "tp"),
            P(None, "tp"),
            P("tp", None, None),
            P("tp", None, None),
            P("tp", None),
            P("tp", None),
            P("tp", "groups", None, None),
            P("groups"),
            P("groups"),
            P("groups", None),
            P("groups"),
        ),
        out_specs=P("role", "groups", "tp"),
        check_vma=False,
    )
```

profile of v0, /device:TPU:0, one launch (start us, length us, event | category | flops | bytes accessed | tf_op | source)
XLA Modules:
  0.0 630.2 jit_solution(2411053265637678212)
XLA Ops:
  6.5 0.0 all-gather.6.cloned.1.call-start
  6.5 7.1 %copy.117 = bf16[1,1024,16,256]{3,2,1,0:T(8,128)(2,1)} copy(bf16[1,1024,16,256]{3,2,1,0:T(8,128)(2,1)} %param.25) | data formatting | bytes 16777216
  13.7 0.0 all-gather.6.cloned.1.call-update
  13.7 7.3 %all-to-all-start.1 = ((bf16[8,8,1024]{2,0,1:T(8,128)(2,1)}), bf16[8,8,1024]{2,0,1:T(8,128)(2,1)S(1)}, u32[]{:S(2)}, u32[]{:S(2)}) async-start(bf16[8,8,1024]{2,0,1:T(8,128)(2,1)} %bitcast.31), calls=%async_computation.1 | async-start | bytes 262144 | tf_op jit(solution)/shard_map/all_to_all | solution.py:167
  21.0 0.0 copy-start.7
  21.0 0.0 copy-start.3
  21.0 0.0 copy-start.6
  21.0 0.0 copy-start
  21.1 5.8 copy.76
  26.9 1.6 all-to-all-done.1
  28.5 0.0 copy-start.4
  28.5 0.0 copy-start.2
  28.5 4.7 all-to-all-start
  33.1 0.0 copy-start.5
  33.2 0.0 copy-start.8
  33.2 0.0 all-gather.4.cloned.1.call-start
  33.2 0.0 copy-done.7
  33.2 0.1 copy.64
  33.4 0.3 shift_right_arithmetic.68
  33.7 0.0 copy-done.3
  33.7 0.0 copy-done.6
  33.7 0.1 multiply_reduce_fusion
  33.8 0.1 compare_select_fusion.2
  33.9 0.1 reshape.345
  34.0 0.0 copy-done
  34.0 1.9 gather_fusion.1
  35.9 0.1 reshape.344
  36.0 0.1 copy.66
  36.1 0.0 copy-done.4
  36.1 0.0 copy-done.2
  36.1 3.3 fusion.56
  39.4 0.0 copy-done.5
  39.4 0.1 pad_add_fusion
  39.5 0.1 select_reduce_fusion.1
  39.6 0.0 copy-done.8
  39.6 0.1 select_convert_fusion
  39.7 0.1 fusion.72
  39.8 0.5 multiply_cosine_fusion
  40.3 168.6 %all-to-all-done = s32[128,8,1024]{0,2,1:T(8,128)} async-done(((s32[128,8,1024]{0,2,1:T(8,128)}), s32[128,8,1024]{0,2,1:T(8,128)}, u32[]{:S(2)}, u32[]{:S(2)}) %all-to-all-start) | async-done | bytes 4194336 | tf_op jit(solution)/shard_map/all_to_all | solution.py:166
  209.0 5.4 copy.77
  214.4 17.7 %fusion.43 = (bf16[8192,1024]{1,0:T(8,128)(2,1)}, bf16[8192,1024]{1,0:T(8,128)(2,1)}) fusion(f32[64,1024]{1,0:T(8,128)S(1)} %convert_bitcast_fusion, s32[1024,1024]{1,0:T(8,128)} %bitcast.137, s32[8192]{0:T(1024)S(1)} %shift_right_arithmetic.68, f32[64,1024]{1,0:T(8,128)S(1)} %convert_element_type.93, s32[1024,1024]{1,0:T(8,128)} %param.19), kind=kLoop, calls=%fused_computation.53 | loop fusion | flops 100663296 | bytes 42500096 | tf_op jit(solution)/shard_map/convert_element_type | solution.py:21
  232.1 21.3 %copy.84 = bf16[1024,8192]{1,0:T(8,128)(2,1)} copy(bf16[1024,8192]{0,1:T(8,128)(2,1)} %bitcast.136) | data formatting | bytes 33554432 | tf_op jit(solution)/shard_map/dot_general | solution.py:148
  253.3 0.0 all-gather.6.cloned.1.call-done
  253.3 0.0 copy-start.1
  253.3 5.3 fusion.51
  258.6 0.5 copy-done.1
  259.1 5.1 fusion.61
  264.2 0.6 fusion.69
  264.8 1.5 collective-permute-start
  266.3 12.3 %fusion.54 = f32[512,8,128]{0,2,1:T(8,128)S(1)} fusion(bf16[8,128,8192]{2,1,0:T(8,128)(2,1)} %bitcast.138, bf16[1,512,8192]{2,1,0:T(8,128)(2,1)S(1)} %copy-done.1, f32[8192]{0:T(1024)S(1)} %convert_element_type.84, f32[512]{0:T(512)S(1)} %add_rsqrt_fusion), kind=kOutput, calls=%fused_computation.69 | convolution fusion | flops 8606711808 | bytes 27297792 | tf_op jit(solution)/shard_map/dot_general | solution.py:148
  278.6 0.4 subtract_convert_fusion
  279.0 0.1 pad_maximum_fusion
  279.1 0.0 collective-permute-done
  279.1 10.4 %conditional.1 = (bf16[512,8,128]{2,0,1:T(8,128)(2,1)S(1)}) conditional(s32[]{:T(128)} %convert_element_type.82, (bf16[1,1024,16,256]{3,2,1,0:T(8,128)(2,1)}, s32[32]{0:T(128)S(1)}, bf16[512,256]{0,1:T(8,128)(2,1)S(1)}, s32[512]{0:T(512)S(1)}, bf16[512,8,128]{0,2,1:T(8,128)(2,1)S(1)}, /*index=5*/s32[512,16]{0,1:T(8,128)S(1)}, ...), branch_computations={%region_3.9_spmd, %region_9.13_spmd} | conditional | flops 1087651840 | bytes 90089912 | solution.py:164
  279.2 0.2 fusion.8
  279.4 5.2 fusion.75
  284.6 4.7 fusion.7
  289.5 1.3 copy.75
  290.8 0.0 all-gather.4.cloned.1.call-update
  290.8 316.9 %all-gather.4.cloned.1.call-done = bf16[512,8192]{0,1:T(8,128)(2,1)} async-done(((bf16[512,1024]{0,1:T(8,128)(2,1)}), bf16[512,8192]{0,1:T(8,128)(2,1)}) %all-gather.4.cloned.1.call-update) | async-done | bytes 8388624 | tf_op jit(solution)/shard_map/all_gather | solution.py:171
  607.8 15.6 %fusion.63 = bf16[1,512,1024]{2,1,0:T(8,128)(2,1)} fusion(bf16[512,8192]{0,1:T(8,128)(2,1)} %all-gather.4.cloned.1.call-done, bf16[8192,1024]{1,0:T(8,128)(2,1)} %get-tuple-element.209), kind=kOutput, calls=%fused_computation.79 | convolution fusion | flops 8590458880 | bytes 26214400 | tf_op jit(solution)/shard_map/dot_general | solution.py:170
  (17 shorter events, 0.3 us)
Async XLA Ops:
  6.5 246.8 %all-gather.6.cloned.1.call-start = ((), (), s32[]{:S(2)}) async-start(), calls=%async_computation.3 | async-start | bytes 9437184 | tf_op jit(solution)/shard_map/all_gather | solution.py:139
  13.7 14.8 %all-to-all-start.1 = ((bf16[8,8,1024]{2,0,1:T(8,128)(2,1)}), bf16[8,8,1024]{2,0,1:T(8,128)(2,1)S(1)}, u32[]{:S(2)}, u32[]{:S(2)}) async-start(bf16[8,8,1024]{2,0,1:T(8,128)(2,1)} %bitcast.31), calls=%async_computation.1 | async-start | bytes 262144 | tf_op jit(solution)/shard_map/all_to_all | solution.py:167
  21.0 12.2 %copy-start.7 = (s32[16]{0:T(128)S(1)}, s32[16]{0:T(128)}, u32[]{:S(2)}) copy-start(s32[16]{0:T(128)} %param.26) | copy-start | bytes 196
  21.0 12.6 %copy-start.3 = (bf16[64,1024]{1,0:T(8,128)(2,1)S(1)}, bf16[64,1024]{1,0:T(8,128)(2,1)}, u32[]{:S(2)}) copy-start(bf16[64,1024]{1,0:T(8,128)(2,1)} %param.20) | copy-start | bytes 393220
  21.0 12.7 %copy-start.6 = (bf16[8192]{0:T(1024)(128)(2,1)S(1)}, bf16[8192]{0:T(1024)(128)(2,1)}, u32[]{:S(2)}) copy-start(bf16[8192]{0:T(1024)(128)(2,1)} %param.18) | copy-start | bytes 49156
  21.0 13.0 %copy-start = (s32[32]{0:T(128)S(1)}, s32[32]{0:T(128)}, u32[]{:S(2)}) copy-start(s32[32]{0:T(128)} %param.27) | copy-start | bytes 388
  28.5 7.6 %copy-start.4 = (bf16[1,64,256]{2,1,0:T(8,128)(2,1)S(1)}, bf16[1,64,256]{2,1,0:T(8,128)(2,1)}, u32[]{:S(2)}) copy-start(bf16[1,64,256]{2,1,0:T(8,128)(2,1)} %param.22) | copy-start | bytes 98308
  28.5 7.6 %copy-start.2 = (s32[1,1024,256]{2,1,0:T(8,128)S(1)}, s32[1,1024,256]{2,1,0:T(8,128)}, u32[]{:S(2)}) copy-start(s32[1,1024,256]{2,1,0:T(8,128)} %param.21) | copy-start | bytes 3145732
  28.5 180.5 %all-to-all-start = ((s32[128,8,1024]{0,2,1:T(8,128)}), s32[128,8,1024]{0,2,1:T(8,128)}, u32[]{:S(2)}, u32[]{:S(2)}) async-start(s32[128,8,1024]{0,2,1:T(8,128)} %bitcast.139), calls=%async_computation | async-start | bytes 8388608 | tf_op jit(solution)/shard_map/all_to_all | solution.py:166
  33.1 6.3 copy-start.5
  33.2 6.4 %copy-start.8 = (s32[496]{0:T(512)S(1)}, s32[496]{0:T(512)}, u32[]{:S(2)}) copy-start(s32[496]{0:T(512)} %param.29) | copy-start | bytes 5956
  33.2 574.6 %all-gather.4.cloned.1.call-start = ((), (), s32[]{:S(2)}) async-start(), calls=%async_computation.2 | async-start | bytes 9437184 | tf_op jit(solution)/shard_map/all_gather | solution.py:171
  253.3 5.8 copy-start.1
  264.8 14.3 %collective-permute-start = (bf16[512,256]{0,1:T(8,128)(2,1)S(1)}, bf16[512,256]{0,1:T(8,128)(2,1)S(1)}, u32[]{:S(2)}, u32[]{:S(2)}) collective-permute-start(bf16[512,256]{0,1:T(8,128)(2,1)S(1)} %pad_maximum_fusion.1), channel_id=1, source_target_pairs={{0,1},{2,3},{4,5},{6,7},{8,9},{10,11},{12,13},{14,15},{16,17},{18,... | collective-permute-start | bytes 786440 | tf_op jit(solution)/shard_map/ppermute | solution.py:12
Sparse Core Ops, SparseCore 0:
  13.8 207.2 all-gather.5
  290.9 316.7 all-gather.3
where the time goes:
time: 632 us; the launch traced here: 630 us
  waiting for transfers between devices  487 us (77%)
  local copies, waits for them, and re-layouts  44 us (7%)
  matrix products  42.8 us (7%)
  other arithmetic  28.7 us (5%)
  between operations  13.7 us (2%)
  starting transfers between devices  13.6 us (2%)
    all_gather x1, waiting for transfers between devices, local(): lax.all_gather(attention_output, 'tp', axis=1, tiled=True)  317 us
    all_to_all x1, waiting for transfers between devices, local(): lax.all_to_all(o_words, 'tp', split_axis=1, concat_axis=0, tiled=True)  169 us
    dot_general x1, local copies, waits for them, and re-layouts, local(): projected = jnp.dot(normed, w_query, preferred_element_type=jnp.float32)  21.3 us
    convert_element_type x2, other arithmetic, unpack_words(): return (values * spread).astype(jnp.bfloat16)  21 us
    dot_general x1, matrix products, local(): jnp.dot(lax.all_gather(attention_output, 'tp', axis=1, tiled=True), w_col...  15.6 us
    unnamed x20, local copies, waits for them, and re-layouts  13.5 us
  transfers between devices with their start and end apart: 5, of which 3 were waited for; matrix products, arithmetic and copies ran while one was open for 11% of the time, Pallas kernels for 0%

commit v1 on v0

--- a/solution.py
+++ b/solution.py
@@ -168,7 +168,7 @@
     )
     w_columns = unpack_words(column_words, column_scales)
     summed = jnp.dot(
-        lax.all_gather(attention_output, "tp", axis=1, tiled=True),
+        jnp.concatenate(lax.all_gather(attention_output, "tp"), axis=1),
         w_columns,
         preferred_element_type=jnp.float32,
     )

time: 632 us -> 577 us (0.913); the launches traced: 630 us -> 568 us
  waiting for transfers between devices: 487 us -> 406 us
  local copies, waits for them, and re-layouts: 44 us -> 63.1 us
    all_to_all x1, waiting for transfers between devices: 169 us -> 50 us  [local(): lax.all_to_all(o_words, 'tp', split_axis=1, concat_axis=0, tiled=True)]
    all_gather x1, waiting for transfers between devices: 0.01 us -> 87.4 us  [local(): whole = lax.all_gather(rows_in[0], 'tp', axis=1, tiled=True)]
    all_gather x1, waiting for transfers between devices: 317 us -> 267 us  [local(): lax.all_gather(attention_output, 'tp')]
    all_gather x0 -> x1, local copies, waits for them, and re-layouts: none -> 11.4 us  [local(): lax.all_gather(attention_output, 'tp')]
    shift_right_arithmetic x2 -> x5, local copies, waits for them, and re-layouts: 0.29 us -> 7.57 us  [unpack_words(): jnp.right_shift(words[:, None, :], shifts[None, :, None])]
    convert_element_type x2 -> x3, other arithmetic: 21 us -> 24.6 us  [unpack_words(): return (values * spread).astype(jnp.bfloat16)]
    unnamed x20 -> x24, local copies, waits for them, and re-layouts: 13.5 us -> 13.3 us
  transfers between devices with their start and end apart: 5 -> 5, of which waited for: 3 -> 4; matrix products, arithmetic and copies ran while one was open for 11% -> 14% of each run, Pallas kernels for 0% -> 0%
where the time goes in v1:
time: 577 us; the launch traced here: 568 us
  waiting for transfers between devices  406 us (70%)
  local copies, waits for them, and re-layouts  63.1 us (11%)
  matrix products  42.8 us (7%)
  other arithmetic  32.3 us (6%)
  between operations  13.7 us (2%)
  starting transfers between devices  9.68 us (2%)
    all_gather x1, waiting for transfers between devices, local(): lax.all_gather(attention_output, 'tp')  267 us
    all_gather x1, waiting for transfers between devices, local(): whole = lax.all_gather(rows_in[0], 'tp', axis=1, tiled=True)  87.4 us
    all_to_all x1, waiting for transfers between devices, local(): lax.all_to_all(o_words, 'tp', split_axis=1, concat_axis=0, tiled=True)  50 us
    convert_element_type x3, other arithmetic, unpack_words(): return (values * spread).astype(jnp.bfloat16)  24.6 us
    dot_general x1, local copies, waits for them, and re-layouts, local(): projected = jnp.dot(normed, w_query, preferred_element_type=jnp.float32)  21.4 us
    dot_general x1, matrix products, local(): jnp.dot(jnp.concatenate(lax.all_gather(attention_output, 'tp'), axis=1),...  15.6 us
    unnamed x24, local copies, waits for them, and re-layouts  13.3 us
    dot_general x1, matrix products, local(): projected = jnp.dot(normed, w_query, preferred_element_type=jnp.float32)  12.3 us
  transfers between devices with their start and end apart: 5, of which 4 were waited for; matrix products, arithmetic and copies ran while one was open for 14% of the time, Pallas kernels for 0%

profile of v1, /device:TPU:0, one launch (start us, length us, event | category | flops | bytes accessed | tf_op | source)
XLA Modules:
  0.0 567.8 jit_solution(13126002758650348179)
XLA Ops:
  6.5 0.0 copy-start.9
  6.5 0.0 all-gather.6.cloned.1.call-start
  6.5 7.2 %copy.118 = bf16[1,1024,16,256]{3,2,1,0:T(8,128)(2,1)} copy(bf16[1,1024,16,256]{3,2,1,0:T(8,128)(2,1)} %param.25) | data formatting | bytes 16777216
  13.7 0.0 all-gather.6.cloned.1.call-update
  13.7 0.0 all-gather.4.cloned.1.call-start
  13.8 0.0 copy-done.9
  13.8 0.1 copy.63
  13.9 0.1 multiply_reduce_fusion
  14.0 0.1 compare_select_fusion.2
  14.1 0.1 reshape.384
  14.2 0.0 copy-done
  14.2 1.9 gather_fusion.1
  16.1 0.1 reshape.383
  16.2 0.1 copy.65
  16.3 0.0 copy-done.6
  16.3 0.0 copy-done.3
  16.3 0.0 copy-start.7
  16.4 0.3 shift_right_arithmetic.75
  16.6 11.3 %fusion.48 = bf16[8192,1024]{1,0:T(8,128)(2,1)} fusion(f32[64,1024]{1,0:T(8,128)S(1)} %convert_element_type.109, s32[8192]{0:T(1024)S(1)} %shift_right_arithmetic.75, s32[1024,1024]{1,0:T(8,128)} %param.19), kind=kLoop, calls=%fused_computation.59 | loop fusion | flops 50331648 | bytes 21266432 | tf_op jit(solution)/shard_map/convert_element_type | solution.py:21
  27.9 0.0 copy-done.7
  28.0 0.0 copy-start.5
  28.0 0.0 copy-start.10
  28.0 21.4 %copy.85 = bf16[1024,8192]{1,0:T(8,128)(2,1)} copy(bf16[1024,8192]{0,1:T(8,128)(2,1)} %bitcast.141) | data formatting | bytes 33554432 | tf_op jit(solution)/shard_map/dot_general | solution.py:148
  49.3 0.0 copy-done.4
  49.4 0.0 copy-done.2
  49.4 3.4 fusion.57
  52.8 0.0 copy-done.5
  52.8 0.1 pad_add_fusion
  52.8 0.1 select_reduce_fusion.1
  52.9 0.0 copy-done.10
  52.9 0.1 select_convert_fusion
  53.0 0.1 fusion.73
  53.1 0.5 multiply_cosine_fusion
  53.6 87.4 %all-gather.6.cloned.1.call-done = bf16[1,512,8192]{2,1,0:T(8,128)(2,1)} async-done(((bf16[1,512,1024]{2,1,0:T(8,128)(2,1)}), bf16[1,512,8192]{2,1,0:T(8,128)(2,1)}) %all-gather.6.cloned.1.call-update) | async-done | bytes 8388624 | tf_op jit(solution)/shard_map/all_gather | solution.py:139
  141.1 5.3 fusion.52
  146.3 0.5 copy-done.1
  146.8 5.1 fusion.62
  152.0 0.6 fusion.70
  152.6 1.5 collective-permute-start
  154.1 12.3 %fusion.55 = f32[512,8,128]{0,2,1:T(8,128)S(1)} fusion(bf16[8,128,8192]{2,1,0:T(8,128)(2,1)} %bitcast.143, bf16[1,512,8192]{2,1,0:T(8,128)(2,1)S(1)} %copy-done.1, f32[8192]{0:T(1024)S(1)} %convert_element_type.100, f32[512]{0:T(512)S(1)} %add_rsqrt_fusion), kind=kOutput, calls=%fused_computation.69 | convolution fusion | flops 8606711808 | bytes 27297792 | tf_op jit(solution)/shard_map/dot_general | solution.py:148
  166.4 0.4 subtract_convert_fusion
  166.7 0.1 pad_maximum_fusion
  166.8 0.0 collective-permute-done
  166.8 10.1 %conditional.1 = (bf16[512,8,128]{2,0,1:T(8,128)(2,1)S(1)}) conditional(s32[]{:T(128)} %convert_element_type.98, (bf16[1,1024,16,256]{3,2,1,0:T(8,128)(2,1)}, s32[32]{0:T(128)S(1)}, bf16[512,256]{0,1:T(8,128)(2,1)S(1)}, s32[512]{0:T(512)S(1)}, bf16[512,8,128]{0,2,1:T(8,128)(2,1)S(1)}, /*index=5*/s32[512,16]{0,1:T(8,128)S(1)}, ...), branch_computations={%region_3.9_spmd, %region_9.13_spmd} | conditional | flops 1087651840 | bytes 90089928 | solution.py:164
  166.9 0.2 fusion.8
  167.1 5.2 fusion.76
  172.3 4.7 fusion.7
  177.0 0.5 copy.74
  177.5 1.3 copy.75
  178.8 0.0 all-gather.4.cloned.1.call-update
  178.8 3.6 all-to-all-start.1
  182.5 0.0 copy-start.8
  182.5 5.6 copy.77
  188.1 1.4 all-to-all-done.1
  189.5 4.5 all-to-all-start
  194.1 0.0 copy-done.8
  194.1 0.1 shift_right_arithmetic.86
  194.2 50.0 %all-to-all-done = s32[128,8,1024]{0,2,1:T(8,128)} async-done(((s32[128,8,1024]{0,2,1:T(8,128)}), s32[128,8,1024]{0,2,1:T(8,128)}, u32[]{:S(2)}, u32[]{:S(2)}) %all-to-all-start) | async-done | bytes 4194336 | tf_op jit(solution)/shard_map/all_to_all | solution.py:166
  244.2 5.4 copy.78
  249.6 7.2 %shift_right_arithmetic.83 = s32[1024,8,1024]{2,1,0:T(8,128)S(1)} broadcast(s32[1024,1024]{1,0:T(8,128)} %bitcast.142), dimensions={0,2} | broadcast | bytes 37748736 | tf_op jit(solution)/shard_map/shift_right_arithmetic | solution.py:17
  256.8 9.9 %fusion.47 = bf16[64,128,1024]{2,1,0:T(8,128)(2,1)} fusion(f32[64,1024]{1,0:T(8,128)S(1)} %convert_bitcast_fusion, s32[128]{0:T(128)S(1)} %shift_right_arithmetic.86, s32[64,128,1024]{2,1,0:T(8,128)S(1)} %bitcast.140), kind=kLoop, calls=%fused_computation.57 | loop fusion | flops 50331648 | bytes 50594304 | tf_op jit(solution)/shard_map/convert_element_type | solution.py:21
  266.7 267.2 %all-gather.4.cloned.1.call-done = bf16[8,512,1024]{2,1,0:T(8,128)(2,1)} async-done(((bf16[1,512,1024]{2,1,0:T(8,128)(2,1)}), bf16[8,512,1024]{2,1,0:T(8,128)(2,1)}) %all-gather.4.cloned.1.call-update) | async-done | bytes 8388624 | tf_op jit(solution)/shard_map/all_gather | solution.py:171
  533.9 11.4 %copy.76 = bf16[8,512,1024]{1,2,0:T(8,128)(2,1)} copy(bf16[8,512,1024]{2,1,0:T(8,128)(2,1)} %all-gather.4.cloned.1.call-done) | data formatting | bytes 16777216 | tf_op jit(solution)/shard_map/all_gather | solution.py:171
  545.3 15.6 %fusion.64 = bf16[1,512,1024]{2,1,0:T(8,128)(2,1)} fusion(bf16[512,8192]{0,1:T(8,128)(2,1)} %bitcast.146, bf16[8192,1024]{1,0:T(8,128)(2,1)} %bitcast.144), kind=kOutput, calls=%fused_computation.79 | convolution fusion | flops 8590458880 | bytes 26214400 | tf_op jit(solution)/shard_map/dot_general | solution.py:170
  (24 shorter events, 0.3 us)
Async XLA Ops:
  6.5 7.3 %copy-start.9 = (s32[16]{0:T(128)S(1)}, s32[16]{0:T(128)}, u32[]{:S(2)}) copy-start(s32[16]{0:T(128)} %param.26) | copy-start | bytes 196
  6.5 7.7 %copy-start = (s32[32]{0:T(128)S(1)}, s32[32]{0:T(128)}, u32[]{:S(2)}) copy-start(s32[32]{0:T(128)} %param.27) | copy-start | bytes 388
  6.5 134.5 %all-gather.6.cloned.1.call-start = ((), (), s32[]{:S(2)}) async-start(), calls=%async_computation.3 | async-start | bytes 9437184 | tf_op jit(solution)/shard_map/all_gather | solution.py:139
  13.7 2.6 copy-start.6
  13.7 2.6 copy-start.3
  13.7 520.2 %all-gather.4.cloned.1.call-start = ((), (), s32[]{:S(2)}) async-start(), calls=%async_computation.2 | async-start | bytes 9437184 | tf_op jit(solution)/shard_map/all_gather | solution.py:171
  16.3 11.6 %copy-start.7 = (s32[8]{0:T(128)}, s32[8]{0:T(128)S(1)}, u32[]{:S(2)}) copy-start(s32[8]{0:T(128)S(1)} %iota_multiply_fusion.1) | copy-start | bytes 100
  27.9 21.4 %copy-start.4 = (bf16[1,64,256]{2,1,0:T(8,128)(2,1)S(1)}, bf16[1,64,256]{2,1,0:T(8,128)(2,1)}, u32[]{:S(2)}) copy-start(bf16[1,64,256]{2,1,0:T(8,128)(2,1)} %param.22) | copy-start | bytes 98308
  27.9 21.4 %copy-start.2 = (s32[1,1024,256]{2,1,0:T(8,128)S(1)}, s32[1,1024,256]{2,1,0:T(8,128)}, u32[]{:S(2)}) copy-start(s32[1,1024,256]{2,1,0:T(8,128)} %param.21) | copy-start | bytes 3145732
  28.0 24.8 %copy-start.5 = (s32[496,16]{0,1:T(8,128)S(1)}, s32[496,16]{0,1:T(8,128)}, u32[]{:S(2)}) copy-start(s32[496,16]{0,1:T(8,128)} %param.28) | copy-start | bytes 95236
  28.0 25.0 %copy-start.10 = (s32[496]{0:T(512)S(1)}, s32[496]{0:T(512)}, u32[]{:S(2)}) copy-start(s32[496]{0:T(512)} %param.29) | copy-start | bytes 5956
  141.1 5.8 %copy-start.1 = (bf16[1,512,8192]{2,1,0:T(8,128)(2,1)S(1)}, bf16[1,512,8192]{2,1,0:T(8,128)(2,1)}, u32[]{:S(2)}) copy-start(bf16[1,512,8192]{2,1,0:T(8,128)(2,1)} %all-gather.6.cloned.1.call-done) | copy-start | bytes 25165828
  152.6 14.3 %collective-permute-start = (bf16[512,256]{0,1:T(8,128)(2,1)S(1)}, bf16[512,256]{0,1:T(8,128)(2,1)S(1)}, u32[]{:S(2)}, u32[]{:S(2)}) collective-permute-start(bf16[512,256]{0,1:T(8,128)(2,1)S(1)} %pad_maximum_fusion.1), channel_id=1, source_target_pairs={{0,1},{2,3},{4,5},{6,7},{8,9},{10,11},{12,13},{14,15},{16,17},{18,... | collective-permute-start | bytes 786440 | tf_op jit(solution)/shard_map/ppermute | solution.py:12
  178.8 10.7 %all-to-all-start.1 = ((bf16[8,8,1024]{2,0,1:T(8,128)(2,1)}), bf16[8,8,1024]{2,0,1:T(8,128)(2,1)S(1)}, u32[]{:S(2)}, u32[]{:S(2)}) async-start(bf16[8,8,1024]{2,0,1:T(8,128)(2,1)} %bitcast.33), calls=%async_computation.1 | async-start | bytes 262144 | tf_op jit(solution)/shard_map/all_to_all | solution.py:167
  182.5 11.6 %copy-start.8 = (s32[8]{0:T(128)S(1)}, s32[8]{0:T(128)}, u32[]{:S(2)}) copy-start(s32[8]{0:T(128)} %copy-done.7) | copy-start | bytes 100
  189.5 54.7 %all-to-all-start = ((s32[128,8,1024]{0,2,1:T(8,128)}), s32[128,8,1024]{0,2,1:T(8,128)}, u32[]{:S(2)}, u32[]{:S(2)}) async-start(s32[128,8,1024]{0,2,1:T(8,128)} %bitcast.145), calls=%async_computation | async-start | bytes 8388608 | tf_op jit(solution)/shard_map/all_to_all | solution.py:166
Sparse Core Ops, SparseCore 0:
  13.9 127.1 all-gather.5
  179.0 354.9 all-gather.3
